TPU v7x, 32 devices: a whole 2x2x4 slice. The times are simulated.
32 devices in a mesh: grp: 2 (over y), sp: 4 (over z), sub: 2 (over x), rep: 2 (over core).
Axes of the slice: x: 2, y: 2, z: 4, core: 2. Of those that a mesh axis runs over, the one named last changes fastest.
Arguments:
- field: float32 [512, 32, 32, 128], P(('grp', 'sp', 'rep'), 'sub'), parts along dimension 0, may hold values from -40 to 40, as said below
- mix_weight: float32 [256, 256], replicated, may hold values from -0.375 to 0.375
- factor_x: float32 [256, 32], replicated, may hold values from -6 to 6
- factor_y: float32 [256, 32], replicated, may hold values from -6 to 6
- factor_z: float32 [256, 32], replicated, may hold values from -6 to 6
- norm_gain: float32 [256], replicated, may hold values from 0.5 to 1.5
- norm_bias: float32 [256], replicated, may hold values from -3 to 3
- w_in: float32 [256, 256], replicated, may hold values from -0.375 to 0.375
- b_in: float32 [256], replicated, may hold values from -3 to 3
- w_out: float32 [256, 256], replicated, may hold values from -0.375 to 0.375
- b_out: float32 [256], replicated, may hold values from -3 to 3
Outputs:
- block_out: float32 [512, 32, 32, 128], P('grp', 'sub', ('sp', 'rep')), parts along dimension 0
There are 2 independent parts, one for each index of `grp`. A program takes and returns all parts, laid end to end along the dimension named above; an argument that names none is the same for every part. Nothing has to cross between parts.
Inputs may be any that keep to these rules, and one draw needn't show every extreme that they name: `field`: real values of order one in each channel, with scales that differ between channels.
All inputs are finite; a program needn't handle non-finite values.
Results may differ from a plain program's by a relative error of at most 0.000078.
Values sent between devices are 32-bit elements; how exact they have to be, the bound alone decides.
A program may use at most 128 MiB of HBM per device.

v0:
```python
import math

import jax
import jax.numpy as jnp
from jax import lax
from jax.sharding import PartitionSpec as P

C = 256
KX = 32
KY = 32
KZ = 32
GROUPS = 32
NX = 32
NY = 32
NZ = 128


def contract(formula, left, right):
    return jnp.einsum(formula, left, right, precision=lax.Precision.HIGHEST)


def tables(length, kept_count):
    indices = jnp.arange(kept_count, dtype=jnp.int32)
    kept_freq = jnp.where(indices < kept_count // 2, indices, length - kept_count + indices)
    positions = jnp.arange(length, dtype=jnp.int32)
    phases = kept_freq[:, None] * positions[None, :] % length
    angles = 2.0 * math.pi / length * phases.astype(jnp.float32)
    return (jnp.cos(angles), jnp.sin(angles))


def transform(planes, cosine, sine, formula):
    real_part = contract(formula, planes[0], cosine) + contract(formula, planes[1], sine)
    imag_part = contract(formula, planes[1], cosine) - contract(formula, planes[0], sine)
    return jnp.stack([real_part, imag_part])


def forward_z(values, cos_z, sin_z):
    return jnp.stack(
        [
            contract("cxyz,kz->ckxy", values, cos_z / NZ),
            -contract("cxyz,kz->ckxy", values, sin_z / NZ),
        ]
    )


def local(
    field, mix_weight, factor_x, factor_y, factor_z, norm_gain, norm_bias, w_in, b_in, w_out, b_out
):
    cos_x, sin_x = tables(NX, KX)
    cos_y, sin_y = tables(NY, KY)
    cos_z, sin_z = tables(NZ, KZ)
    wide_count = lax.axis_size(("sp", "rep"))
    narrow_count = lax.axis_size("sub")
    x_local = NX // narrow_count
    y_local = NY // wide_count
    ky_local = KY // narrow_count
    kz_local = KZ // wide_count
    x_cos = (cos_x / NX).reshape(KX, narrow_count, x_local)
    x_sin = (sin_x / NX).reshape(KX, narrow_count, x_local)
    spatial = lax.all_to_all(field, ("sp", "rep"), split_axis=2, concat_axis=0, tiled=True)
    planes = forward_z(spatial, cos_z, sin_z)
    planes = planes.reshape(2, C, -1)
    planes = lax.all_to_all(planes, ("sp", "rep"), split_axis=2, concat_axis=2, tiled=True)
    planes = planes.reshape(2, C, wide_count, kz_local, x_local, y_local)
    y_cos = (cos_y / NY).reshape(KY, wide_count, y_local)
    y_sin = (sin_y / NY).reshape(KY, wide_count, y_local)
    planes = transform(planes, y_cos, y_sin, "cskxy,jsy->cjkx")
    planes = planes.reshape(2, C, -1)
    planes = lax.all_to_all(planes, "sub", split_axis=2, concat_axis=2, tiled=True)
    planes = planes.reshape(2, C, narrow_count, ky_local, kz_local, x_local)
    spectra = transform(planes, x_cos, x_sin, "csjkx,isx->ckji")
    spectra = spectra.reshape(2, C, -1)
    factor_ky = lax.dynamic_slice_in_dim(factor_y, lax.axis_index("sub") * ky_local, ky_local, 1)
    factor_kz = lax.dynamic_slice_in_dim(
        factor_z, lax.axis_index(("sp", "rep")) * kz_local, kz_local, 1
    )
    weighting = (
        factor_kz[:, :, None, None] * factor_ky[:, None, :, None] * factor_x[:, None, None, :]
    )
    weighting = weighting.reshape(C, -1)
    mixed_modes = contract("oc,rcm->rom", mix_weight, spectra * weighting[None])
    mixed_modes = mixed_modes.reshape(2, C, kz_local, ky_local, KX)
    returned = transform(mixed_modes, cos_x, -sin_x, "ckji,ix->cxkj")
    returned = returned.reshape(2, C, -1)
    returned = lax.all_to_all(returned, "sub", split_axis=2, concat_axis=2, tiled=True)
    returned = returned.reshape(2, C, narrow_count, x_local, kz_local, ky_local)
    back_cos = cos_y.reshape(narrow_count, ky_local, NY)
    back_sin = (-sin_y).reshape(narrow_count, ky_local, NY)
    returned = transform(returned, back_cos, back_sin, "csxkj,sjy->cyxk")
    returned = returned.reshape(2, C, -1)
    returned = lax.all_to_all(returned, ("sp", "rep"), split_axis=2, concat_axis=2, tiled=True)
    returned = returned.reshape(2, C, wide_count, y_local, x_local, kz_local)
    z_cos = cos_z.reshape(wide_count, kz_local, NZ)
    z_sin = sin_z.reshape(wide_count, kz_local, NZ)
    spectral = contract("csyxk,skz->cxyz", returned[0], z_cos) - contract(
        "csyxk,skz->cxyz", returned[1], z_sin
    )
    summed = spatial + spectral
    columns = summed.reshape(C, -1)
    cells_group = C // GROUPS * NX * NY * NZ
    grouped = columns.reshape(GROUPS, -1)
    first_sum, second_sum = lax.psum(
        (jnp.sum(grouped, axis=1), jnp.sum(grouped * grouped, axis=1)), ("sp", "sub", "rep")
    )
    group_mean = first_sum / cells_group
    group_var = second_sum / cells_group - group_mean * group_mean
    inv_scale = jnp.repeat(lax.rsqrt(group_var + 1e-05), C // GROUPS) * norm_gain
    mean_chan = jnp.repeat(group_mean, C // GROUPS)
    normed = (columns - mean_chan[:, None]) * inv_scale[:, None] + norm_bias[:, None]
    hidden = jax.nn.gelu(jnp.dot(w_in, normed, precision=lax.Precision.HIGHEST) + b_in[:, None])
    result = columns + jnp.dot(w_out, hidden, precision=lax.Precision.HIGHEST) + b_out[:, None]
    return result.reshape(summed.shape)


def solution(mesh):
    placed = (
        P(("grp", "sp", "rep"), "sub", None, None),
        P(),
        P(),
        P(),
        P(),
        P(),
        P(),
        P(),
        P(),
        P(),
        P(),
    )
    return jax.shard_map(
        local,
        mesh=mesh,
        in_specs=placed,
        out_specs=P("grp", "sub", ("sp", "rep"), None),
        check_vma=False,
    )
```

profile of v0, /device:TPU:0, one launch (start us, length us, event | category | flops | bytes accessed | tf_op | source)
XLA Modules:
  0.0 806.4 jit_solution(14237701336524410925)
XLA Ops:
  0.0 11.7 %copy.45 = f32[32,16,32,128]{3,1,0,2:T(8,128)} copy(f32[32,16,32,128]{3,2,1,0:T(8,128)} %param.11) | data formatting | bytes 16777216 | tf_op args[0]
  11.7 6.5 all-to-all-start
  18.2 183.8 %all-to-all-done = f32[32,16,32,128]{3,1,0,2:T(8,128)} async-done(((f32[32,16,32,128]{3,1,0,2:T(8,128)}), f32[32,16,32,128]{3,1,0,2:T(8,128)}, u32[]{:S(2)}, u32[]{:S(2)}) %all-to-all-start) | async-done | bytes 8388640 | tf_op jit(solution)/shard_map/all_to_all | solution.py:60
  202.0 6.1 copy.46
  208.1 8.7 %negate_bitcast_fusion = f32[256,32,16,4]{0,1,3,2:T(8,128)S(1)} fusion(f32[256,16,4,128]{3,0,2,1:T(8,128)S(1)} %bitcast.259, s32[32]{0:T(128)S(1)} %compare_select_fusion.1), kind=kOutput, calls=%fused_computation.50 | convolution fusion | flops 805892096 | bytes 10485888 | tf_op jit(solution)/shard_map/cxyz,kz->ckxy/dot_general | solution.py:19
  216.8 10.3 %convolution_bitcast_fusion.1 = f32[256,32,16,4]{0,1,3,2:T(8,128)} fusion(f32[256,16,4,128]{3,0,2,1:T(8,128)S(1)} %bitcast.260, s32[32]{0:T(128)S(1)} %compare_select_fusion.1), kind=kOutput, calls=%fused_computation.59 | convolution fusion | flops 805367808 | bytes 10485888 | tf_op jit(solution)/shard_map/cxyz,kz->ckxy/dot_general | solution.py:19
  230.2 2.9 copy.47
  234.9 2.5 pad_maximum_fusion
  237.4 12.2 %copy.49 = f32[2,256,2048]{1,0,2:T(2,128)} copy(f32[2,256,2048]{1,2,0:T(8,128)S(1)} %pad_maximum_fusion) | data formatting | bytes 8388608 | tf_op jit(solution)/shard_map/stack | solution.py:38
  249.6 4.7 all-to-all-start.1
  254.4 94.0 %all-to-all-done.1 = f32[2,256,2048]{1,0,2:T(2,128)} async-done(((f32[2,256,2048]{1,0,2:T(2,128)}), f32[2,256,2048]{1,0,2:T(2,128)}, u32[]{:S(2)}, u32[]{:S(2)}) %all-to-all-start.1) | async-done | bytes 4194336 | tf_op jit(solution)/shard_map/all_to_all | solution.py:63
  348.3 15.3 %slice_reduce_fusion.3 = (f32[256,2048]{0,1:T(8,128)}, f32[256,2048]{0,1:T(8,128)}) fusion(f32[2,256,2048]{1,0,2:T(2,128)} %all-to-all-done.1), kind=kLoop, calls=%fused_computation.31 | loop fusion | bytes 8388608 | tf_op jit(solution)/shard_map/slice | solution.py:32
  365.5 4.4 fusion.26
  369.9 4.4 fusion.28
  374.2 2.1 squeeze.38
  376.3 4.8 fusion.24
  381.2 3.1 fusion.23
  387.0 12.2 %copy.56 = f32[2,256,2048]{1,0,2:T(2,128)} copy(f32[2,256,2048]{1,2,0:T(8,128)S(1)} %pad_maximum_fusion.1) | data formatting | bytes 8388608 | tf_op jit(solution)/shard_map/stack | solution.py:34
  399.3 5.7 all-to-all-start.2
  406.0 46.4 %all-to-all-done.2 = f32[2,256,2048]{1,0,2:T(2,128)} async-done(((f32[2,256,2048]{1,0,2:T(2,128)}), f32[2,256,2048]{1,0,2:T(2,128)}, u32[]{:S(2)}, u32[]{:S(2)}) %all-to-all-start.2) | async-done | bytes 4194336 | tf_op jit(solution)/shard_map/all_to_all | solution.py:69
  452.4 7.3 fusion.233
  460.0 2.1 fusion.63
  462.0 2.1 fusion.61
  464.1 2.1 fusion.19
  466.2 2.1 fusion.18
  469.4 3.7 fusion.15
  484.0 10.5 %copy.67 = f32[2,256,2048]{1,0,2:T(2,128)S(1)} copy(f32[2,256,2048]{1,2,0:T(8,128)S(1)} %pad_maximum_fusion.2) | data formatting | bytes 8388608 | tf_op jit(solution)/shard_map/stack | solution.py:34
  494.4 49.4 %all_to_all.38 = f32[2,256,2048]{1,0,2:T(2,128)S(1)} all-to-all(f32[2,256,2048]{1,0,2:T(2,128)S(1)} %copy.67), channel_id=1, replica_groups=mesh['grp'=2,'sp'=4,'sub'=2,'rep'=2] {'sub'}, dimensions={2} | all-to-all | bytes 8388608 | tf_op jit(solution)/shard_map/all_to_all | solution.py:85
  543.8 3.3 fusion.231
  551.5 2.1 fusion.17
  553.7 2.1 fusion.16
  555.8 2.7 copy.75
  558.4 3.4 stack.58
  561.8 2.7 copy.72
  564.4 3.1 stack.57
  569.4 12.2 %copy.76 = f32[2,256,2048]{1,0,2:T(2,128)} copy(f32[2,256,2048]{1,2,0:T(8,128)S(1)} %pad_maximum_fusion.3) | data formatting | bytes 8388608 | tf_op jit(solution)/shard_map/stack | solution.py:34
  581.6 4.5 all-to-all-start.4
  586.2 94.0 %all-to-all-done.4 = f32[2,256,2048]{1,0,2:T(2,128)} async-done(((f32[2,256,2048]{1,0,2:T(2,128)}), f32[2,256,2048]{1,0,2:T(2,128)}, u32[]{:S(2)}, u32[]{:S(2)}) %all-to-all-start.4) | async-done | bytes 4194336 | tf_op jit(solution)/shard_map/all_to_all | solution.py:91
  680.2 15.3 %slice_reduce_fusion = (f32[256,2048]{0,1:T(8,128)}, f32[256,2048]{0,1:T(8,128)}) fusion(f32[2,256,2048]{1,0,2:T(2,128)} %all-to-all-done.4), kind=kLoop, calls=%fused_computation.28 | loop fusion | bytes 8388608 | tf_op jit(solution)/shard_map/slice | solution.py:96
  697.3 3.0 squeeze.46
  700.4 15.2 %fusion.21 = f32[128,256,4,16,1]{0,1,4,2,3:T(8,128)S(1)} fusion(f32[256,8,4,16,4]{0,4,3,2,1:T(4,128)} %squeeze.46, s32[8,4]{0,1:T(4,128)S(1)} %compare_select_fusion), kind=kOutput, calls=%fused_computation.41 | convolution fusion | flops 805363712 | bytes 10485888 | tf_op jit(solution)/shard_map/csyxk,skz->cxyz/dot_general | solution.py:19
  715.5 17.4 %fusion.230 = (f32[256]{0:T(256)S(1)}, f32[256]{0:T(256)S(1)}, f32[256,16,4,128]{3,0,2,1:T(8,128)}) fusion(f32[256,16,4,128]{3,0,2,1:T(8,128)} %bitcast.261, f32[256,8,4,16,4]{0,4,3,2,1:T(4,128)S(1)} %squeeze.47, s32[8,4]{0,1:T(4,128)S(1)} %compare_select_fusion, f32[128,256,4,16,1]{0,1,4,2,3:T(8,128)S(1)} %fusion.21), kind=kOutput, calls=%fused_computation.266 | convolution fusion | flops 815848960 | bytes 27265152 | tf_op jit(solution)/shard_map/csyxk,skz->cxyz/dot_general | solution.py:19
  733.3 30.2 %all-reduce = (f32[32]{0:T(128)S(1)}, f32[32]{0:T(128)S(1)}) all-reduce(f32[32]{0:T(128)S(1)} %reduce_sum.37, f32[32]{0:T(128)S(1)} %reduce_sum.25), channel_id=1, replica_groups=mesh['grp'=2,'sp'=4,'sub'=2,'rep'=2] {'sp','sub','rep'}, use_global_device_ids=true, to_apply=%region_5.6 | all-reduce | flops 64 | bytes 512 | tf_op jit(solution)/shard_map/psum | solution.py:102
  763.9 9.3 %copy.81 = f32[256,16,4,128]{0,3,2,1:T(8,128)} copy(f32[256,16,4,128]{3,0,2,1:T(8,128)} %get-tuple-element.21) | data formatting | bytes 16777216 | tf_op jit(solution)/shard_map/add | solution.py:98
  773.2 4.4 fusion.11
  777.7 8.7 %fusion.9 = f32[256,8192]{0,1:T(8,128)S(1)} fusion(f32[256,8192]{0,1:T(8,128)S(1)} %fusion.11, f32[256,256]{1,0:T(8,128)S(1)} %copy-done, f32[256]{0:T(256)S(1)} %copy-done.11), kind=kOutput, calls=%fused_computation.12 | convolution fusion | flops 6461325312 | bytes 17040384 | tf_op jit(solution)/shard_map/dot_general | solution.py:110
  786.4 9.3 %fusion.1 = f32[256,8192]{0,1:T(8,128)} fusion(f32[256,8192]{0,1:T(8,128)S(1)} %bitcast.264, f32[256,8192]{0,1:T(8,128)S(1)} %fusion.9, f32[256,256]{1,0:T(8,128)S(1)} %copy-done.4, f32[256]{0:T(256)S(1)} %copy-done.8), kind=kOutput, calls=%fused_computation.3 | convolution fusion | flops 6446645248 | bytes 25428992 | tf_op jit(solution)/shard_map/dot_general | solution.py:111
  795.7 10.2 %copy.82 = f32[256,16,4,128]{3,2,1,0:T(4,128)} copy(f32[256,16,4,128]{0,3,2,1:T(8,128)} %bitcast.265) | data formatting | bytes 16777216 | tf_op jit(solution)/shard_map/reshape | solution.py:112
  (72 shorter events, 31.5 us)
Async XLA Ops:
  0.0 777.6 %copy-start = (f32[256,256]{1,0:T(8,128)S(1)}, f32[256,256]{1,0:T(8,128)}, u32[]{:S(2)}) copy-start(f32[256,256]{1,0:T(8,128)} %param.18) | copy-start | bytes 786436
  11.7 190.3 %all-to-all-start = ((f32[32,16,32,128]{3,1,0,2:T(8,128)}), f32[32,16,32,128]{3,1,0,2:T(8,128)}, u32[]{:S(2)}, u32[]{:S(2)}) async-start(f32[32,16,32,128]{3,1,0,2:T(8,128)} %copy.45), calls=%async_computation | async-start | bytes 16777216 | tf_op jit(solution)/shard_map/all_to_all | solution.py:60
  208.1 8.7 %copy-start.1 = (f32[32,16,8,4,128]{4,0,2,3,1:T(8,128)}, f32[32,16,8,4,128]{4,0,2,3,1:T(8,128)S(1)}, u32[]{:S(2)}) copy-start(f32[32,16,8,4,128]{4,0,2,3,1:T(8,128)S(1)} %copy.46) | copy-start | bytes 25165828
  249.6 98.7 %all-to-all-start.1 = ((f32[2,256,2048]{1,0,2:T(2,128)}), f32[2,256,2048]{1,0,2:T(2,128)}, u32[]{:S(2)}, u32[]{:S(2)}) async-start(f32[2,256,2048]{1,0,2:T(2,128)} %copy.49), calls=%async_computation.1 | async-start | bytes 8388608 | tf_op jit(solution)/shard_map/all_to_all | solution.py:63
  376.3 4.9 copy-start.2
  399.3 6.5 copy-start.7
  399.3 6.5 copy-start.6
  399.3 53.1 %all-to-all-start.2 = ((f32[2,256,2048]{1,0,2:T(2,128)}), f32[2,256,2048]{1,0,2:T(2,128)}, u32[]{:S(2)}, u32[]{:S(2)}) async-start(f32[2,256,2048]{1,0,2:T(2,128)} %copy.56), calls=%async_computation.2 | async-start | bytes 8388608 | tf_op jit(solution)/shard_map/all_to_all | solution.py:69
  468.5 1.0 copy-start.5
  564.4 3.1 copy-start.3
  581.6 98.5 %all-to-all-start.4 = ((f32[2,256,2048]{1,0,2:T(2,128)}), f32[2,256,2048]{1,0,2:T(2,128)}, u32[]{:S(2)}, u32[]{:S(2)}) async-start(f32[2,256,2048]{1,0,2:T(2,128)} %copy.76), calls=%async_computation.4 | async-start | bytes 8388608 | tf_op jit(solution)/shard_map/all_to_all | solution.py:91
  763.8 9.3 %copy-start.10 = (f32[256]{0:T(256)S(1)}, f32[256]{0:T(256)}, u32[]{:S(2)}) copy-start(f32[256]{0:T(256)} %param.16) | copy-start | bytes 3076
  763.8 9.3 %copy-start.9 = (f32[256]{0:T(256)S(1)}, f32[256]{0:T(256)}, u32[]{:S(2)}) copy-start(f32[256]{0:T(256)} %param.17) | copy-start | bytes 3076
  773.2 4.5 copy-start.11
  773.2 13.2 %slice-start = ((s8[8388608]{0:T(1024)(128)(4,1)}), s8[4194304]{0:T(1024)(128)(4,1)S(1)}, s32[]{:S(2)}) async-start(s8[8388608]{0:T(1024)(128)(4,1)} %bitcast.262), calls=%async_computation.5 | async-start | bytes 8388608
  777.6 8.7 %slice-start.1 = ((s8[8388608]{0:T(1024)(128)(4,1)}), s8[4194304]{0:T(1024)(128)(4,1)S(1)}, s32[]{:S(2)}) async-start(s8[8388608]{0:T(1024)(128)(4,1)} %bitcast.262), calls=%async_computation.6 | async-start | bytes 8388608
  777.7 8.7 %copy-start.4 = (f32[256,256]{1,0:T(8,128)S(1)}, f32[256,256]{1,0:T(8,128)}, u32[]{:S(2)}) copy-start(f32[256,256]{1,0:T(8,128)} %param.20) | copy-start | bytes 786436
  777.7 8.7 %copy-start.8 = (f32[256]{0:T(256)S(1)}, f32[256]{0:T(256)}, u32[]{:S(2)}) copy-start(f32[256]{0:T(256)} %param.21) | copy-start | bytes 3076
where the time goes:
time: 812 us; the launch traced here: 806 us
  waiting for transfers between devices  418 us (51%)
  local copies, waits for them, and re-layouts  162 us (20%)
  matrix products  114 us (14%)
  blocking collectives  79.5 us (10%)
  starting transfers between devices  21.5 us (3%)
  other arithmetic  9.88 us (1%)
    all_to_all x1, waiting for transfers between devices, local(): lax.all_to_all(field, ('sp', 'rep'), split_axis=2, concat_axis=0, tiled=T...  184 us
    dot_general x21, matrix products, contract(): return jnp.einsum(formula, left, right, precision=lax.Precision.HIGHEST)  96.4 us
    all_to_all x1, waiting for transfers between devices, local(): lax.all_to_all(returned, ('sp', 'rep'), split_axis=2, concat_axis=2, tile...  94 us
    all_to_all x1, waiting for transfers between devices, local(): lax.all_to_all(planes, ('sp', 'rep'), split_axis=2, concat_axis=2, tiled=...  94 us
    all_to_all x1, blocking collectives, local(): lax.all_to_all(returned, 'sub', split_axis=2, concat_axis=2, tiled=True)  49.4 us
    all_to_all x1, waiting for transfers between devices, local(): lax.all_to_all(planes, 'sub', split_axis=2, concat_axis=2, tiled=True)  46.4 us
    another operation x5, local copies, waits for them, and re-layouts, transform(): return jnp.stack([real_part, imag_part])  41.4 us
    psum x1, blocking collectives, local(): lax.psum((jnp.sum(grouped, axis=1), jnp.sum(grouped * grouped, axis=1)),...  30.2 us
  transfers between devices with their start and end apart: 4, of which 4 were waited for; matrix products, arithmetic and copies ran while one was open for 0% of the time, Pallas kernels for 0%

commit v1 on v0

v1 whole, which is shorter than its diff:
```python
import math
import functools

import jax
import jax.numpy as jnp
from jax import lax
from jax.experimental import pallas as pl
from jax.experimental.pallas import tpu as pltpu
from jax.sharding import PartitionSpec as P

GROUPS = 32
HIGH = lax.Precision.HIGH
WIDE = ("sp", "rep")


def trig(length, freq, positions):
    phases = (freq[:, None] * positions[None, :]) % length
    angles = 2.0 * math.pi / length * phases.astype(jnp.float32)
    return jnp.cos(angles), jnp.sin(angles)


def kron_pair(cos_a, sin_a, cos_b, sin_b):
    ca, sa = cos_a.T[:, None, :, None], sin_a.T[:, None, :, None]
    cb, sb = cos_b.T[None, :, None, :], sin_b.T[None, :, None, :]
    return ca * cb - sa * sb, sa * cb + ca * sb


def split(value):
    high = value.astype(jnp.bfloat16)
    low = (value - high.astype(jnp.float32)).astype(jnp.bfloat16)
    return high, low


def dot3(left, right):
    lh, ll = left
    rh, rl = right
    d = functools.partial(jnp.dot, preferred_element_type=jnp.float32)
    return d(lh, rh) + (d(lh, rl) + d(ll, rh))


def sum_kernel(field_ref, modes_ref, table_ref, summed_ref, first_ref, second_ref, acc1, acc2):
    step = pl.program_id(0)
    chans, cells, width = field_ref.shape
    rank = modes_ref.shape[2]

    @pl.when(step == 0)
    def _():
        acc1[...] = jnp.zeros_like(acc1)
        acc2[...] = jnp.zeros_like(acc2)

    table = split(table_ref[...])
    chunk = 32 if chans % 32 == 0 else chans

    def body(index, carry):
        rows = pl.ds(pl.multiple_of(index * chunk, chunk), chunk)
        modes = modes_ref[rows].reshape(chunk * cells, rank)
        value = dot3(split(modes), table).reshape(chunk, cells, width) + field_ref[rows]
        summed_ref[rows] = value
        acc1[rows] += value
        acc2[rows] += value * value
        return carry

    lax.fori_loop(0, chans // chunk, body, 0)

    @pl.when(step == pl.num_programs(0) - 1)
    def _():
        first_ref[...] = jnp.sum(acc1[...], axis=1)
        second_ref[...] = jnp.sum(acc2[...], axis=1)


def mlp_kernel(summed_ref, vec_ref, w_in_ref, w_out_ref, out_ref):
    cells = summed_ref.shape[1]
    w_in = split(w_in_ref[...])
    w_out = split(w_out_ref[...])
    vec = vec_ref[...]
    mean, scale, bias = vec[:, 0:1], vec[:, 1:2], vec[:, 2:3]
    b_in, b_out = vec[:, 3:4], vec[:, 4:5]
    pair = 2 if cells % 2 == 0 else 1
    for start in range(0, cells, pair):
        parts = [summed_ref[:, p, :] for p in range(start, start + pair)]
        value = jnp.concatenate(parts, axis=1) if pair > 1 else parts[0]
        normed = (value - mean) * scale + bias
        hidden = dot3(w_in, split(normed)) + b_in
        inner = math.sqrt(2.0 / math.pi) * (hidden + 0.044715 * (hidden * hidden * hidden))
        hidden = hidden * (0.5 * (1.0 + jnp.tanh(inner)))
        result = value + dot3(w_out, split(hidden)) + b_out
        width = summed_ref.shape[2]
        for k in range(pair):
            out_ref[:, start + k, :] = result[:, k * width : (k + 1) * width]


def local(
    field, mix_weight, factor_x, factor_y, factor_z, norm_gain, norm_bias, w_in, b_in, w_out, b_out
):
    wide_count = lax.axis_size(WIDE)
    narrow_count = lax.axis_size("sub")
    own_chans, x_local, ny, nz = field.shape
    chans = own_chans * wide_count
    nx = x_local * narrow_count
    kx, ky, kz = factor_x.shape[1], factor_y.shape[1], factor_z.shape[1]
    y_local = ny // wide_count
    half = kz // 2
    kept = half + 1
    me_sub = lax.axis_index("sub")
    cells = x_local * y_local

    spatial = lax.all_to_all(field, WIDE, split_axis=2, concat_axis=0, tiled=True)

    cos_z, sin_z = trig(nz, jnp.arange(kept), jnp.arange(nz))
    forward = jnp.concatenate([cos_z, -sin_z]) / nz
    planes = jnp.einsum("rz,cxyz->rcxy", forward, field, precision=HIGH)
    planes = planes.reshape(2 * kept * own_chans, x_local * ny)

    def freqs(length, count):
        index = jnp.arange(count)
        return jnp.where(index < count // 2, index, length - count + index)

    cos_y, sin_y = trig(ny, freqs(ny, ky), jnp.arange(ny))

    def forward_xy(values, owner):
        cos_x, sin_x = trig(nx, freqs(nx, kx), owner * x_local + jnp.arange(x_local))
        c, s = kron_pair(cos_x, sin_x, cos_y, sin_y)
        c = (c / (nx * ny)).reshape(x_local * ny, kx * ky)
        s = (s / (nx * ny)).reshape(x_local * ny, kx * ky)
        a = jnp.dot(values, jnp.concatenate([c, s], axis=1), precision=HIGH)
        a = a.reshape(2, kept * own_chans, 2, kx * ky)
        return a[0, :, 0] + a[1, :, 1], a[1, :, 0] - a[0, :, 1]

    held = planes
    real, imag = forward_xy(held, me_sub)
    for hop in range(1, narrow_count):
        held = lax.ppermute(held, "sub", [(i, (i + 1) % narrow_count) for i in range(narrow_count)])
        owner = (me_sub - hop + narrow_count) % narrow_count
        more_real, more_imag = forward_xy(held, owner)
        real, imag = real + more_real, imag + more_imag

    start = lax.axis_index(WIDE) * own_chans
    fx = lax.dynamic_slice_in_dim(factor_x, start, own_chans, 0)
    fy = lax.dynamic_slice_in_dim(factor_y, start, own_chans, 0)
    fz = lax.dynamic_slice_in_dim(factor_z, start, own_chans, 0)
    mirror_x = (-jnp.arange(kx)) % kx
    mirror_y = (-jnp.arange(ky)) % ky
    plane_a = (fx[:, :, None] * fy[:, None, :]).reshape(own_chans, kx * ky)
    plane_b = (fx[:, mirror_x][:, :, None] * fy[:, mirror_y][:, None, :]).reshape(own_chans, kx * ky)
    zero = jnp.zeros((own_chans, 1), jnp.float32)
    z_plus = jnp.concatenate([fz[:, :half], zero], axis=1).T
    z_minus = jnp.concatenate([zero, fz[:, half:][:, ::-1]], axis=1).T
    weight = z_plus[:, :, None] * plane_a[None] + z_minus[:, :, None] * plane_b[None]
    weight = weight.reshape(kept * own_chans, kx * ky)
    real, imag = real * weight, imag * weight

    cos_x, sin_x = trig(nx, freqs(nx, kx), me_sub * x_local + jnp.arange(x_local))
    c, s = kron_pair(cos_x, sin_x, cos_y, sin_y)

    def columns(t):
        t = t.reshape(x_local, wide_count, y_local, kx * ky)
        return t.transpose(3, 1, 0, 2).reshape(kx * ky, wide_count * cells)

    c, s = columns(c), columns(s)
    table_re = jnp.concatenate([c, -s])
    table_im = jnp.concatenate([s, c])
    both = jnp.concatenate([real, imag], axis=1)
    back = jnp.stack(
        [jnp.dot(both, table_re, precision=HIGH), jnp.dot(both, table_im, precision=HIGH)]
    )
    back = back.reshape(2 * kept, own_chans, wide_count, cells)
    back = back.transpose(2, 1, 0, 3).reshape(wide_count * own_chans, 2 * kept * cells)
    back = lax.all_to_all(back, WIDE, split_axis=0, concat_axis=0, tiled=True)
    back = back.reshape(chans, 2 * kept, cells)
    mixed = jnp.einsum("oi,irp->opr", mix_weight, back, precision=HIGH)

    inverse_z = jnp.concatenate([cos_z, -sin_z])
    spatial = spatial.reshape(chans, cells, nz)
    block = 8 if cells % 8 == 0 else cells
    steps = cells // block
    cube = pl.BlockSpec((chans, block, nz), lambda i: (0, i, 0))
    whole = lambda *shape: pl.BlockSpec(shape, lambda i: (0,) * len(shape))
    summed, first, second = pl.pallas_call(
        sum_kernel,
        grid=(steps,),
        out_shape=(
            jax.ShapeDtypeStruct(spatial.shape, jnp.float32),
            jax.ShapeDtypeStruct((chans, nz), jnp.float32),
            jax.ShapeDtypeStruct((chans, nz), jnp.float32),
        ),
        in_specs=[
            cube,
            pl.BlockSpec((chans, block, 2 * kept), lambda i: (0, i, 0)),
            whole(2 * kept, nz),
        ],
        out_specs=(cube, whole(chans, nz), whole(chans, nz)),
        scratch_shapes=[pltpu.VMEM((chans, block, nz), jnp.float32)] * 2,
        name="sum_stats",
    )(spatial, mixed, inverse_z)

    size = chans // GROUPS
    stats = jnp.stack([first, second]).reshape(2, GROUPS, size * nz).sum(axis=2)
    everyone = ("sp", "sub", "rep")
    stats = lax.all_gather(stats, everyone).reshape(-1, 2, GROUPS).sum(axis=0)
    cells_group = size * nx * ny * nz
    group_mean = stats[0] / cells_group
    group_var = stats[1] / cells_group - group_mean * group_mean
    scale = jnp.repeat(lax.rsqrt(group_var + 1e-05), size) * norm_gain
    mean = jnp.repeat(group_mean, size)
    vec = jnp.stack([mean, scale, norm_bias, b_in, b_out] + [b_out] * 3, axis=1)

    result = pl.pallas_call(
        mlp_kernel,
        grid=(steps,),
        out_shape=jax.ShapeDtypeStruct(spatial.shape, jnp.float32),
        in_specs=[cube, whole(chans, 8), whole(*w_in.shape), whole(*w_out.shape)],
        out_specs=cube,
        name="mlp",
    )(summed, vec, w_in, w_out)
    return result.reshape(chans, x_local, y_local, nz)


def solution(mesh):
    placed = (P(("grp", "sp", "rep"), "sub", None, None),) + (P(),) * 10
    return jax.shard_map(
        local,
        mesh=mesh,
        in_specs=placed,
        out_specs=P("grp", "sub", ("sp", "rep"), None),
        check_vma=False,
    )
```

time: 812 us -> 500 us (0.62)
  waiting for transfers between devices: 418 us -> 207 us
  matrix products: 114 us -> 42.9 us
  blocking collectives: 79.5 us -> 18.4 us
  Pallas kernels: 0 us -> 36.5 us
  local copies, waits for them, and re-layouts: 162 us -> 143 us
  other arithmetic: 9.88 us -> 28.5 us
  starting transfers between devices: 21.5 us -> 13.1 us
    all_to_all x4 -> x2, waiting for transfers between devices: 418 us -> 207 us  [the longest x1 167 us: local(): lax.all_to_all(field, WIDE, split_axis=2, concat_axis=0, tiled=True)]
    dot_general x23 -> x6, matrix products: 114 us -> 42.9 us  [the longest x2 21.3 us: forward_xy(): a = jnp.dot(values, jnp.concatenate([c, s], axis=1), precision=HIGH)]
    another operation x8 -> x5, local copies, waits for them, and re-layouts: 57.2 us -> 2.77 us  [the longest x2 1.86 us: local(): stats = jnp.stack([first, second]).reshape(2, GROUPS, size * nz).sum(axis=2)]
    all_to_all x1 -> x0, blocking collectives: 49.4 us -> none  [local(): lax.all_to_all(returned, 'sub', split_axis=2, concat_axis=2, tiled=True)]
    pallas_call x0 -> x2, Pallas kernels: none -> 36.5 us  [the longest x1 19.2 us: local(): pl.pallas_call(mlp_kernel, grid=(steps,), out_shape=jax.ShapeDtypeStruct(...]
    psum x1 -> x0, blocking collectives: 30.2 us -> none  [local(): lax.psum((jnp.sum(grouped, axis=1), jnp.sum(grouped * grouped, axis=1)),...]
    div x0 -> x4, local copies, waits for them, and re-layouts: none -> 29.5 us  [the longest x2 14.9 us: forward_xy(): s = (s / (nx * ny)).reshape(x_local * ny, kx * ky)]
    slice x5 -> x2, local copies, waits for them, and re-layouts: 41.4 us -> 12.7 us  [the longest x1 12.7 us: forward_xy(): return (a[0, :, 0] + a[1, :, 1], a[1, :, 0] - a[0, :, 1])]
  transfers between devices with their start and end apart: 4 -> 3, of which waited for: 4 -> 2; matrix products, arithmetic and copies ran while one was open for 0% -> 22% of each run, Pallas kernels for 0% -> 0%
where the time goes in v1:
time: 500 us; the launch traced here: 490 us
  waiting for transfers between devices  207 us (41%)
  local copies, waits for them, and re-layouts  143 us (29%)
  matrix products  42.9 us (9%)
  Pallas kernels  36.5 us (7%)
  other arithmetic  28.5 us (6%)
  blocking collectives  18.4 us (4%)
  starting transfers between devices  13.1 us (3%)
    all_to_all x1, waiting for transfers between devices, local(): lax.all_to_all(field, WIDE, split_axis=2, concat_axis=0, tiled=True)  167 us
    all_to_all x1, waiting for transfers between devices, local(): back = lax.all_to_all(back, WIDE, split_axis=0, concat_axis=0, tiled=True)  40.2 us
    dot_general x2, matrix products, forward_xy(): a = jnp.dot(values, jnp.concatenate([c, s], axis=1), precision=HIGH)  21.3 us
    pallas_call x1, Pallas kernels, local(): pl.pallas_call(mlp_kernel, grid=(steps,), out_shape=jax.ShapeDtypeStruct(...  19.2 us
    all_gather x1, blocking collectives, local(): stats = lax.all_gather(stats, everyone).reshape(-1, 2, GROUPS).sum(axis=0)  18.4 us
    pallas_call x1, Pallas kernels, local(): pl.pallas_call(sum_kernel, grid=(steps,), out_shape=(jax.ShapeDtypeStruct...  17.3 us
    div x2, local copies, waits for them, and re-layouts, forward_xy(): s = (s / (nx * ny)).reshape(x_local * ny, kx * ky)  14.9 us
    div x2, local copies, waits for them, and re-layouts, forward_xy(): c = (c / (nx * ny)).reshape(x_local * ny, kx * ky)  14.7 us
  transfers between devices with their start and end apart: 3, of which 2 were waited for; matrix products, arithmetic and copies ran while one was open for 22% of the time, Pallas kernels for 0%

profile of v1, /device:TPU:0, one launch (start us, length us, event | category | flops | bytes accessed | tf_op | source)
XLA Modules:
  0.0 490.0 jit_solution(7118595710183418558)
XLA Ops:
  0.1 0.6 copy-done.6
  0.7 7.8 %fusion.30 = f32[34,32,16,32]{0,3,2,1:T(8,128)} fusion(f32[32,16,32,128]{3,2,1,0:T(8,128)} %param.11, f32[34,128]{1,0:T(8,128)S(1)} %pad_maximum_fusion.9.table_ref), kind=kOutput, calls=%fused_computation.51 | convolution fusion | flops 427823360 | bytes 10634240 | tf_op jit(solution)/shard_map/rz,cxyz->rcxy/dot_general | solution.py:111
  8.5 10.1 %copy.68 = f32[34,32,16,32]{3,2,1,0:T(8,128)} copy(f32[34,32,16,32]{0,3,2,1:T(8,128)} %fusion.30) | data formatting | bytes 4456448 | tf_op jit(solution)/shard_map/rz,cxyz->rcxy/dot_general | solution.py:111
  18.6 7.5 %reshape.357 = f32[1088,512]{1,0:T(8,128)} reshape(f32[34,32,16,32]{3,2,1,0:T(8,128)} %copy.68) | data formatting | bytes 4456448 | tf_op jit(solution)/shard_map/reshape | solution.py:112
  26.1 3.0 collective-permute-start
  30.1 12.2 %subtract_multiply_fusion = (f32[16,32,32,32]{1,0,3,2:T(8,128)}, f32[16,32,32,32]{1,0,3,2:T(8,128)}, f32[16,32,32,32]{1,0,3,2:T(8,128)}, f32[16,32,32,32]{1,0,3,2:T(8,128)}) fusion(f32[16,32]{0,1:T(8,128)S(1)} %copy.75, f32[16,32]{0,1:T(8,128)S(1)} %copy.74, f32[32,32]{0,1:T(8,128)S(1)} %copy.72, f32[32,32]{0,1:T(8,128)S(1)} %copy.70, f32[16,32]{0,1:T(8,128)S(1)} %copy.69, ...), kind=kLoop, calls=%fused_computation.3 | loop fusion | flops 8388608 | bytes 8404992 | tf_op jit(solution)/shard_map/div | solution.py:123
  42.3 6.5 %reshape.384 = f32[2,544,512,1]{2,1,0,3:T(8,128)S(1)} reshape(f32[34,32,16,32]{3,2,1,0:T(8,128)} %copy.68) | data formatting | bytes 4456448 | tf_op jit(solution)/shard_map/dot_general | solution.py:125
  48.9 0.6 gather_fusion
  49.5 0.6 gather_fusion.1
  50.2 7.3 %div.43 = f32[512,1024]{0,1:T(8,128)} reshape(f32[16,32,32,32]{1,0,3,2:T(8,128)} %get-tuple-element.19) | data formatting | bytes 4194304 | tf_op jit(solution)/shard_map/div | solution.py:123
  57.5 7.4 %div.45 = f32[512,1024]{0,1:T(8,128)} reshape(f32[16,32,32,32]{1,0,3,2:T(8,128)} %get-tuple-element.20) | data formatting | bytes 4194304 | tf_op jit(solution)/shard_map/div | solution.py:124
  64.9 7.3 %div.39 = f32[512,1024]{0,1:T(8,128)} reshape(f32[16,32,32,32]{1,0,3,2:T(8,128)} %get-tuple-element.24) | data formatting | bytes 4194304 | tf_op jit(solution)/shard_map/div | solution.py:123
  72.2 7.5 %div.41 = f32[512,1024]{0,1:T(8,128)} reshape(f32[16,32,32,32]{1,0,3,2:T(8,128)} %get-tuple-element.23) | data formatting | bytes 4194304 | tf_op jit(solution)/shard_map/div | solution.py:124
  80.1 0.2 mul.559
  81.2 0.8 mul.566
  82.1 0.8 mul.575
  82.9 0.3 mul.570
  83.2 0.3 mul.579
  83.5 4.1 multiply_add_fusion
  87.6 3.0 add.216
  90.6 3.3 neg.22
  93.9 2.9 sub.36
  96.8 2.7 pad_maximum_fusion.1
  99.5 9.6 %fusion.21 = f32[2,544,2,1024]{3,1,2,0:T(8,128)} fusion(f32[2,1024,512,1]{2,1,0,3:T(8,128)S(1)} %bitcast.110, f32[2,544,512,1]{2,1,0,3:T(8,128)S(1)} %reshape.384), kind=kOutput, calls=%fused_computation.37 | convolution fusion | flops 6845104128 | bytes 15335424 | tf_op jit(solution)/shard_map/dot_general | solution.py:125
  109.1 11.7 %fusion.2 = f32[1088,2048]{1,0:T(8,128)} fusion(f32[1088,512]{1,0:T(8,128)} %collective-permute-done, f32[512,1024]{0,1:T(8,128)S(1)} %copy-done.2, f32[512,1024]{0,1:T(8,128)S(1)} %copy-done.1), kind=kOutput, calls=%fused_computation.11 | convolution fusion | flops 6846152704 | bytes 15335424 | tf_op jit(solution)/shard_map/dot_general | solution.py:125
  120.8 12.5 %reshape.358 = f32[2,544,2,1024]{3,2,1,0:T(2,128)} reshape(f32[1088,2048]{1,0:T(8,128)} %fusion.2) | data formatting | bytes 17825792 | tf_op jit(solution)/shard_map/reshape | solution.py:126
  133.3 12.7 %fusion.74 = (f32[1,544,1,1024]{3,2,1,0:T(1,128)S(1)}, f32[1,544,1,1024]{3,2,1,0:T(1,128)S(1)}, f32[1,544,1,1024]{3,2,1,0:T(1,128)S(1)}, f32[1,544,1,1024]{3,2,1,0:T(1,128)S(1)}) fusion(f32[2,544,2,1024]{3,2,1,0:T(2,128)} %reshape.358), kind=kLoop, calls=%fused_computation.119 | loop fusion | bytes 17825792 | tf_op jit(solution)/shard_map/slice | solution.py:127
  146.0 4.9 fusion.19
  150.9 3.8 fusion.23
  154.7 3.8 fusion.26
  158.7 2.5 reshape.359
  161.3 7.2 %copy.105 = f32[34,32,8,64]{3,0,1,2:T(8,128)} copy(f32[34,32,8,64]{3,2,1,0:T(8,128)} %reshape.359) | data formatting | bytes 4456448 | tf_op jit(solution)/shard_map/reshape | solution.py:166
  168.5 4.8 all_to_all.20
  173.3 4.9 all-to-all-start.1
  178.2 11.6 %copy.66 = f32[32,16,32,128]{3,1,0,2:T(8,128)} copy(f32[32,16,32,128]{3,2,1,0:T(8,128)} %param.11) | data formatting | bytes 16777216 | tf_op args[0]
  189.9 40.2 %all-to-all-done.1 = f32[8,32,2176]{2,1,0:T(8,128)S(1)} async-done(((f32[8,32,2176]{2,1,0:T(8,128)}), f32[8,32,2176]{2,1,0:T(8,128)S(1)}, u32[]{:S(2)}, u32[]{:S(2)}) %all-to-all-start.1) | async-done | bytes 2228256 | tf_op jit(solution)/shard_map/all_to_all | solution.py:168
  230.1 5.3 %all-to-all-start = ((f32[32,16,32,128]{3,1,0,2:T(8,128)}), f32[32,16,32,128]{3,1,0,2:T(8,128)}, u32[]{:S(2)}, u32[]{:S(2)}) async-start(f32[32,16,32,128]{3,1,0,2:T(8,128)} %copy.66), calls=%async_computation | async-start | bytes 16777216 | tf_op jit(solution)/shard_map/all_to_all | solution.py:107
  235.3 3.1 reshape.360
  238.5 6.1 %fusion = f32[34,64,256]{2,1,0:T(8,128)S(1)} fusion(f32[256,34,64]{2,1,0:T(8,128)} %reshape.360, f32[256,256]{1,0:T(8,128)S(1)} %copy-done), kind=kOutput, calls=%fused_computation.8 | convolution fusion | flops 855638016 | bytes 4718592 | tf_op jit(solution)/shard_map/oi,irp->opr/dot_general | solution.py:170
  244.6 7.7 %copy.86 = f32[34,64,256]{0,1,2:T(8,128)} copy(f32[34,64,256]{2,1,0:T(8,128)S(1)} %fusion) | data formatting | bytes 4456448 | tf_op jit(solution)/shard_map/oi,irp->opr/dot_general | solution.py:170
  252.3 166.9 %all-to-all-done = f32[32,16,32,128]{3,1,0,2:T(8,128)} async-done(((f32[32,16,32,128]{3,1,0,2:T(8,128)}), f32[32,16,32,128]{3,1,0,2:T(8,128)}, u32[]{:S(2)}, u32[]{:S(2)}) %all-to-all-start) | async-done | bytes 8388640 | tf_op jit(solution)/shard_map/all_to_all | solution.py:107
  419.2 12.3 %copy.67 = f32[32,16,8,4,128]{4,3,1,0,2:T(4,128)} copy(f32[32,16,8,4,128]{4,1,0,3,2:T(8,128)} %bitcast) | data formatting | bytes 16777216 | tf_op jit(solution)/shard_map/all_to_all | solution.py:107
  431.5 17.3 %sum_stats.1 = (f32[256,64,128]{2,1,0:T(8,128)}, f32[256,128]{1,0:T(8,128)}, f32[256,128]{1,0:T(8,128)}) custom-call(f32[256,64,128]{2,1,0:T(8,128)} %bitcast.108, f32[256,64,34]{2,1,0:T(8,128)} %bitcast.107, f32[34,128]{1,0:T(8,128)} %copy-done.6), custom_call_target="tpu_custom_call" | custom-call | tf_op jit(solution)/shard_map/sum_stats/pallas_call | solution.py:178
  448.8 0.9 stack.39
  449.7 0.9 stack.40
  450.8 18.4 %all-gather.1 = f32[16,2,32]{2,1,0:T(2,128)S(1)} all-gather(f32[1,2,32]{2,1,0:T(2,128)S(1)} %bitcast.121), channel_id=2, replica_groups=mesh['grp'=2,'sp'=4,'sub'=2,'rep'=2] {'sp','sub','rep'}, dimensions={0}, use_global_device_ids=true | all-gather | bytes 4352 | tf_op jit(solution)/shard_map/all_gather | solution.py:199
  469.6 0.8 copy.87.vec_ref
  470.4 19.2 %mlp.1 = f32[256,64,128]{2,1,0:T(8,128)} custom-call(f32[256,64,128]{2,1,0:T(8,128)} %get-tuple-element.8.summed_ref, f32[256,8]{1,0:T(8,128)} %copy.87.vec_ref, f32[256,256]{1,0:T(8,128)} %w_in_ref.1, f32[256,256]{1,0:T(8,128)} %w_out_ref.1), custom_call_target="tpu_custom_call" | custom-call | tf_op jit(solution)/shard_map/mlp/pallas_call | solution.py:207
  (75 shorter events, 3.3 us)
Async XLA Ops:
  0.0 238.5 %copy-start = (f32[256,256]{1,0:T(8,128)S(1)}, f32[256,256]{1,0:T(8,128)}, u32[]{:S(2)}) copy-start(f32[256,256]{1,0:T(8,128)} %param.12) | copy-start | bytes 786436
  0.1 0.6 copy-start.6
  18.6 11.4 %copy-start.9 = (f32[256,32]{0,1:T(8,128)S(1)}, f32[256,32]{0,1:T(8,128)}, u32[]{:S(2)}) copy-start(f32[256,32]{0,1:T(8,128)} %param.14) | copy-start | bytes 98308
  18.6 11.4 %copy-start.10 = (f32[256,32]{0,1:T(8,128)S(1)}, f32[256,32]{0,1:T(8,128)}, u32[]{:S(2)}) copy-start(f32[256,32]{0,1:T(8,128)} %param.13) | copy-start | bytes 98308
  26.1 83.0 %collective-permute-start = (f32[1088,512]{1,0:T(8,128)}, f32[1088,512]{1,0:T(8,128)}, u32[]{:S(2)}, u32[]{:S(2)}) collective-permute-start(f32[1088,512]{1,0:T(8,128)} %reshape.357), channel_id=1, source_target_pairs={{0,2},{2,0},{1,3},{3,1},{4,6},{6,4},{5,7},{7,5},{8,10},{10,8},{9,1... | collective-permute-start | bytes 6684680 | tf_op jit(solution)/shard_map/ppermute | solution.py:132
  79.7 1.1 copy-start.8
  79.7 1.2 copy-start.14
  99.4 9.7 %copy-start.1 = (f32[512,1024]{0,1:T(8,128)S(1)}, f32[512,1024]{0,1:T(8,128)}, u32[]{:S(2)}) copy-start(f32[512,1024]{0,1:T(8,128)} %div.43) | copy-start | bytes 6291460
  99.5 9.7 %copy-start.2 = (f32[512,1024]{0,1:T(8,128)S(1)}, f32[512,1024]{0,1:T(8,128)}, u32[]{:S(2)}) copy-start(f32[512,1024]{0,1:T(8,128)} %div.45) | copy-start | bytes 6291460
  146.0 4.9 copy-start.3
  146.0 4.9 copy-start.5
  150.9 3.8 copy-start.4
  173.3 56.7 %all-to-all-start.1 = ((f32[8,32,2176]{2,1,0:T(8,128)}), f32[8,32,2176]{2,1,0:T(8,128)S(1)}, u32[]{:S(2)}, u32[]{:S(2)}) async-start(f32[8,32,2176]{2,1,0:T(8,128)} %all_to_all.20), calls=%async_computation.1 | async-start | bytes 4456448 | tf_op jit(solution)/shard_map/all_to_all | solution.py:168
  230.1 189.1 %all-to-all-start = ((f32[32,16,32,128]{3,1,0,2:T(8,128)}), f32[32,16,32,128]{3,1,0,2:T(8,128)}, u32[]{:S(2)}, u32[]{:S(2)}) async-start(f32[32,16,32,128]{3,1,0,2:T(8,128)} %copy.66), calls=%async_computation | async-start | bytes 16777216 | tf_op jit(solution)/shard_map/all_to_all | solution.py:107
  431.5 38.1 %copy-start.11 = (f32[256]{0:T(256)S(1)}, f32[256]{0:T(256)}, u32[]{:S(2)}) copy-start(f32[256]{0:T(256)} %param.16) | copy-start | bytes 3076
  431.5 38.1 %copy-start.7 = (f32[256]{0:T(256)S(1)}, f32[256]{0:T(256)}, u32[]{:S(2)}) copy-start(f32[256]{0:T(256)} %param.21) | copy-start | bytes 3076
  431.5 38.1 %copy-start.12 = (f32[256]{0:T(256)S(1)}, f32[256]{0:T(256)}, u32[]{:S(2)}) copy-start(f32[256]{0:T(256)} %param.17) | copy-start | bytes 3076
  431.5 38.1 %copy-start.13 = (f32[256]{0:T(256)S(1)}, f32[256]{0:T(256)}, u32[]{:S(2)}) copy-start(f32[256]{0:T(256)} %param.19) | copy-start | bytes 3076

commit v2 on v1

--- a/solution.py
+++ b/solution.py
@@ -165,6 +165,7 @@
     )
     back = back.reshape(2 * kept, own_chans, wide_count, cells)
     back = back.transpose(2, 1, 0, 3).reshape(wide_count * own_chans, 2 * kept * cells)
+    back, spatial = lax.optimization_barrier((back, spatial))
     back = lax.all_to_all(back, WIDE, split_axis=0, concat_axis=0, tiled=True)
     back = back.reshape(chans, 2 * kept, cells)
     mixed = jnp.einsum("oi,irp->opr", mix_weight, back, precision=HIGH)

time: 500 us -> 353 us (0.71)
  waiting for transfers between devices: 207 us -> 13.3 us
  blocking collectives: 18.4 us -> 74.3 us
  starting transfers between devices: 13.1 us -> 8.07 us
    all_to_all x1, waiting for transfers between devices: 167 us -> 13.3 us  [local(): lax.all_to_all(field, WIDE, split_axis=2, concat_axis=0, tiled=True)]
    all_to_all x0 -> x1, blocking collectives: none -> 55 us  [local(): back = lax.all_to_all(back, WIDE, split_axis=0, concat_axis=0, tiled=True)]
    all_to_all x1 -> x0, waiting for transfers between devices: 40.2 us -> none  [local(): back = lax.all_to_all(back, WIDE, split_axis=0, concat_axis=0, tiled=True)]
  transfers between devices with their start and end apart: 3 -> 2, of which waited for: 2 -> 1; matrix products, arithmetic and copies ran while one was open for 22% -> 48% of each run, Pallas kernels for 0% -> 0%
where the time goes in v2:
time: 353 us; the launch traced here: 347 us
  local copies, waits for them, and re-layouts  143 us (41%)
  blocking collectives  74.3 us (21%)
  matrix products  42.9 us (12%)
  Pallas kernels  36.4 us (10%)
  other arithmetic  28.3 us (8%)
  waiting for transfers between devices  13.3 us (4%)
  starting transfers between devices  8.07 us (2%)
    all_to_all x1, blocking collectives, local(): back = lax.all_to_all(back, WIDE, split_axis=0, concat_axis=0, tiled=True)  55 us
    dot_general x2, matrix products, forward_xy(): a = jnp.dot(values, jnp.concatenate([c, s], axis=1), precision=HIGH)  21.3 us
    all_gather x1, blocking collectives, local(): stats = lax.all_gather(stats, everyone).reshape(-1, 2, GROUPS).sum(axis=0)  19.3 us
    pallas_call x1, Pallas kernels, local(): pl.pallas_call(mlp_kernel, grid=(steps,), out_shape=jax.ShapeDtypeStruct(...  19.2 us
    pallas_call x1, Pallas kernels, local(): pl.pallas_call(sum_kernel, grid=(steps,), out_shape=(jax.ShapeDtypeStruct...  17.2 us
    div x2, local copies, waits for them, and re-layouts, forward_xy(): s = (s / (nx * ny)).reshape(x_local * ny, kx * ky)  14.8 us
    div x2, local copies, waits for them, and re-layouts, forward_xy(): c = (c / (nx * ny)).reshape(x_local * ny, kx * ky)  14.7 us
    all_to_all x1, waiting for transfers between devices, local(): lax.all_to_all(field, WIDE, split_axis=2, concat_axis=0, tiled=True)  13.3 us
  transfers between devices with their start and end apart: 2, of which 1 were waited for; matrix products, arithmetic and copies ran while one was open for 48% of the time, Pallas kernels for 0%

profile of v2, /device:TPU:0, one launch (start us, length us, event | category | flops | bytes accessed | tf_op | source)
XLA Modules:
  0.0 347.3 jit_solution(2451606487816585732)
XLA Ops:
  0.0 11.7 %copy.83 = f32[32,16,32,128]{3,1,0,2:T(8,128)} copy(f32[32,16,32,128]{3,2,1,0:T(8,128)} %param.11) | data formatting | bytes 16777216 | tf_op args[0]
  11.7 6.6 %all-to-all-start = ((f32[32,16,32,128]{3,1,0,2:T(8,128)}), f32[32,16,32,128]{3,1,0,2:T(8,128)}, u32[]{:S(2)}, u32[]{:S(2)}) async-start(f32[32,16,32,128]{3,1,0,2:T(8,128)} %copy.83), calls=%async_computation | async-start | bytes 16777216 | tf_op jit(solution)/shard_map/all_to_all | solution.py:107
  18.4 0.6 copy-done.6
  19.0 7.8 %fusion.30 = f32[34,32,16,32]{0,3,2,1:T(8,128)} fusion(f32[32,16,32,128]{3,2,1,0:T(8,128)} %param.11, f32[34,128]{1,0:T(8,128)S(1)} %pad_maximum_fusion.9.table_ref), kind=kOutput, calls=%fused_computation.51 | convolution fusion | flops 427823360 | bytes 10634240 | tf_op jit(solution)/shard_map/rz,cxyz->rcxy/dot_general | solution.py:111
  26.8 10.1 %copy.66 = f32[34,32,16,32]{3,2,1,0:T(8,128)} copy(f32[34,32,16,32]{0,3,2,1:T(8,128)} %fusion.30) | data formatting | bytes 4456448 | tf_op jit(solution)/shard_map/rz,cxyz->rcxy/dot_general | solution.py:111
  36.8 7.5 %reshape.356 = f32[1088,512]{1,0:T(8,128)} reshape(f32[34,32,16,32]{3,2,1,0:T(8,128)} %copy.66) | data formatting | bytes 4456448 | tf_op jit(solution)/shard_map/reshape | solution.py:112
  44.3 1.5 collective-permute-start
  46.8 12.2 %subtract_multiply_fusion = (f32[16,32,32,32]{1,0,3,2:T(8,128)}, f32[16,32,32,32]{1,0,3,2:T(8,128)}, f32[16,32,32,32]{1,0,3,2:T(8,128)}, f32[16,32,32,32]{1,0,3,2:T(8,128)}) fusion(f32[16,32]{0,1:T(8,128)S(1)} %copy.73, f32[16,32]{0,1:T(8,128)S(1)} %copy.72, f32[32,32]{0,1:T(8,128)S(1)} %copy.70, f32[32,32]{0,1:T(8,128)S(1)} %copy.68, f32[16,32]{0,1:T(8,128)S(1)} %copy.67, ...), kind=kLoop, calls=%fused_computation.3 | loop fusion | flops 8388608 | bytes 8404992 | tf_op jit(solution)/shard_map/div | solution.py:123
  59.0 6.5 %reshape.385 = f32[2,544,512,1]{2,1,0,3:T(8,128)S(1)} reshape(f32[34,32,16,32]{3,2,1,0:T(8,128)} %copy.66) | data formatting | bytes 4456448 | tf_op jit(solution)/shard_map/dot_general | solution.py:125
  65.7 0.6 gather_fusion
  66.2 0.6 gather_fusion.1
  66.9 7.3 %div.43 = f32[512,1024]{0,1:T(8,128)} reshape(f32[16,32,32,32]{1,0,3,2:T(8,128)} %get-tuple-element.23) | data formatting | bytes 4194304 | tf_op jit(solution)/shard_map/div | solution.py:123
  74.2 7.3 %div.45 = f32[512,1024]{0,1:T(8,128)} reshape(f32[16,32,32,32]{1,0,3,2:T(8,128)} %get-tuple-element.24) | data formatting | bytes 4194304 | tf_op jit(solution)/shard_map/div | solution.py:124
  81.5 7.3 %div.39 = f32[512,1024]{0,1:T(8,128)} reshape(f32[16,32,32,32]{1,0,3,2:T(8,128)} %get-tuple-element.28) | data formatting | bytes 4194304 | tf_op jit(solution)/shard_map/div | solution.py:123
  88.9 7.5 %div.41 = f32[512,1024]{0,1:T(8,128)} reshape(f32[16,32,32,32]{1,0,3,2:T(8,128)} %get-tuple-element.27) | data formatting | bytes 4194304 | tf_op jit(solution)/shard_map/div | solution.py:124
  96.8 0.2 mul.559
  97.2 0.2 mul.550
  97.9 0.8 mul.566
  98.8 0.8 mul.575
  99.6 0.3 mul.570
  99.9 0.3 mul.579
  100.2 4.0 %multiply_add_fusion = (f32[1024,8,16,4]{0,3,2,1:T(4,128)}, f32[1024,8,16,4]{0,3,2,1:T(4,128)}) fusion(f32[1024,8,4]{0,2,1:T(4,128)S(1)} %bitcast.115, f32[1024,16]{0,1:T(8,128)} %bitcast.117, f32[1024,8,4]{0,2,1:T(4,128)S(1)} %bitcast.114, f32[1024,16]{0,1:T(8,128)} %bitcast.116), kind=kLoop, calls=%fused_computation.39 | loop fusion | flops 3145728 | bytes 4587520 | tf_op jit(solution)/shard_map/add | solution.py:25
  104.2 3.0 add.216
  107.2 3.2 neg.22
  110.4 2.9 sub.36
  113.3 2.7 pad_maximum_fusion.1
  116.0 9.7 %fusion.21 = f32[2,544,2,1024]{3,1,2,0:T(8,128)} fusion(f32[2,1024,512,1]{2,1,0,3:T(8,128)S(1)} %bitcast.112, f32[2,544,512,1]{2,1,0,3:T(8,128)S(1)} %reshape.385), kind=kOutput, calls=%fused_computation.37 | convolution fusion | flops 6845104128 | bytes 15335424 | tf_op jit(solution)/shard_map/dot_general | solution.py:125
  125.7 11.6 %fusion.2 = f32[1088,2048]{1,0:T(8,128)} fusion(f32[1088,512]{1,0:T(8,128)} %collective-permute-done, f32[512,1024]{0,1:T(8,128)S(1)} %copy-done.2, f32[512,1024]{0,1:T(8,128)S(1)} %copy-done.1), kind=kOutput, calls=%fused_computation.11 | convolution fusion | flops 6846152704 | bytes 15335424 | tf_op jit(solution)/shard_map/dot_general | solution.py:125
  137.3 12.5 %reshape.357 = f32[2,544,2,1024]{3,2,1,0:T(2,128)} reshape(f32[1088,2048]{1,0:T(8,128)} %fusion.2) | data formatting | bytes 17825792 | tf_op jit(solution)/shard_map/reshape | solution.py:126
  149.8 12.6 %fusion.74 = (f32[1,544,1,1024]{3,2,1,0:T(1,128)S(1)}, f32[1,544,1,1024]{3,2,1,0:T(1,128)S(1)}, f32[1,544,1,1024]{3,2,1,0:T(1,128)S(1)}, f32[1,544,1,1024]{3,2,1,0:T(1,128)S(1)}) fusion(f32[2,544,2,1024]{3,2,1,0:T(2,128)} %reshape.357), kind=kLoop, calls=%fused_computation.119 | loop fusion | bytes 17825792 | tf_op jit(solution)/shard_map/slice | solution.py:127
  162.4 4.9 %fusion.19 = (f32[544,1024]{1,0:T(8,128)S(1)}, f32[544,1024]{1,0:T(8,128)S(1)}) fusion(f32[2,544,2,1024]{3,1,2,0:T(8,128)} %fusion.21, f32[1,544,1,1024]{3,2,1,0:T(1,128)S(1)} %get-tuple-element.19, f32[1,544,1,1024]{3,2,1,0:T(1,128)S(1)} %get-tuple-element.17, f32[32,1024]{1,0:T(8,128)S(1)} %mul.559, f32[544]{0:T(1024)S(1)} %mul.554, ...), kind=kLoop, calls=%fused_computation.30 | loop fusion | flops 6127616 | bytes 22548736 | tf_op jit(solution)/shard_map/mul | solution.py:150
  167.3 3.8 %fusion.23 = f32[1,544,512]{2,1,0:T(8,128)S(1)} fusion(f32[1024,512]{0,1:T(8,128)S(1)} %copy-done.5, f32[1024,512]{0,1:T(8,128)S(1)} %copy-done.3, f32[544,1024]{1,0:T(8,128)S(1)} %get-tuple-element.16, f32[544,1024]{1,0:T(8,128)S(1)} %get-tuple-element.15), kind=kOutput, calls=%fused_computation.41 | convolution fusion | flops 3424714752 | bytes 9764864 | tf_op jit(solution)/shard_map/dot_general | solution.py:164
  171.2 3.8 %fusion.26 = f32[1,544,512]{2,1,0:T(8,128)S(1)} fusion(f32[1024,512]{0,1:T(8,128)S(1)} %copy-done.4, f32[1024,512]{0,1:T(8,128)S(1)} %copy-done.5, f32[544,1024]{1,0:T(8,128)S(1)} %get-tuple-element.16, f32[544,1024]{1,0:T(8,128)S(1)} %get-tuple-element.15), kind=kOutput, calls=%fused_computation.42 | convolution fusion | flops 3424714752 | bytes 9764864 | tf_op jit(solution)/shard_map/dot_general | solution.py:164
  175.2 2.6 reshape.358
  177.8 7.2 %copy.105 = f32[34,32,8,64]{3,0,1,2:T(8,128)} copy(f32[34,32,8,64]{3,2,1,0:T(8,128)} %reshape.358) | data formatting | bytes 4456448 | tf_op jit(solution)/shard_map/reshape | solution.py:166
  185.0 3.9 %reshape.359 = f32[256,2176]{1,0:T(8,128)S(1)} reshape(f32[8,32,34,64]{3,2,1,0:T(8,128)} %bitcast.111) | data formatting | bytes 4456448 | tf_op jit(solution)/shard_map/reshape | solution.py:167
  188.9 13.3 %all-to-all-done = f32[32,16,32,128]{3,1,0,2:T(8,128)} async-done(((f32[32,16,32,128]{3,1,0,2:T(8,128)}), f32[32,16,32,128]{3,1,0,2:T(8,128)}, u32[]{:S(2)}, u32[]{:S(2)}) %all-to-all-start) | async-done | bytes 8388640 | tf_op jit(solution)/shard_map/all_to_all | solution.py:107
  202.2 12.3 %copy.84 = f32[8,32,16,4,128]{4,3,2,1,0:T(4,128)} copy(f32[8,32,16,4,128]{4,2,1,3,0:T(8,128)} %bitcast.23) | data formatting | bytes 16777216 | tf_op jit(solution)/shard_map/all_to_all | solution.py:107
  214.4 55.0 %all_to_all.27 = f32[8,32,2176]{2,1,0:T(8,128)} all-to-all(f32[8,32,2176]{2,1,0:T(8,128)S(1)} %bitcast.113), channel_id=1, replica_groups=mesh['grp'=2,'sp'=4,'sub'=2,'rep'=2] {'sp','rep'}, dimensions={0} | all-to-all | bytes 4456448 | tf_op jit(solution)/shard_map/all_to_all | solution.py:169
  269.4 4.9 %reshape.361 = f32[256,34,64]{2,1,0:T(8,128)} reshape(f32[8,32,2176]{2,1,0:T(8,128)} %all_to_all.27) | data formatting | bytes 4456448 | tf_op jit(solution)/shard_map/reshape | solution.py:170
  274.3 6.1 %fusion = f32[34,64,256]{2,1,0:T(8,128)S(1)} fusion(f32[256,34,64]{2,1,0:T(8,128)} %reshape.361, f32[256,256]{1,0:T(8,128)S(1)} %copy-done), kind=kOutput, calls=%fused_computation.8 | convolution fusion | flops 855638016 | bytes 4718592 | tf_op jit(solution)/shard_map/oi,irp->opr/dot_general | solution.py:171
  280.5 7.7 %copy.86 = f32[34,64,256]{0,1,2:T(8,128)} copy(f32[34,64,256]{2,1,0:T(8,128)S(1)} %fusion) | data formatting | bytes 4456448 | tf_op jit(solution)/shard_map/oi,irp->opr/dot_general | solution.py:171
  288.1 17.2 %sum_stats.1 = (f32[256,64,128]{2,1,0:T(8,128)}, f32[256,128]{1,0:T(8,128)}, f32[256,128]{1,0:T(8,128)}) custom-call(f32[256,64,128]{2,1,0:T(8,128)} %bitcast.109, f32[256,64,34]{2,1,0:T(8,128)} %bitcast.110, f32[34,128]{1,0:T(8,128)} %copy-done.6), custom_call_target="tpu_custom_call" | custom-call | tf_op jit(solution)/shard_map/sum_stats/pallas_call | solution.py:179
  305.3 0.9 stack.39
  306.2 0.9 stack.40
  307.3 19.3 %all-gather.1 = f32[16,2,32]{2,1,0:T(2,128)S(1)} all-gather(f32[1,2,32]{2,1,0:T(2,128)S(1)} %bitcast.124), channel_id=2, replica_groups=mesh['grp'=2,'sp'=4,'sub'=2,'rep'=2] {'sp','sub','rep'}, dimensions={0}, use_global_device_ids=true | all-gather | bytes 4352 | tf_op jit(solution)/shard_map/all_gather | solution.py:200
  327.1 0.8 copy.87.vec_ref
  327.9 19.2 %mlp.1 = f32[256,64,128]{2,1,0:T(8,128)} custom-call(f32[256,64,128]{2,1,0:T(8,128)} %get-tuple-element.12.summed_ref, f32[256,8]{1,0:T(8,128)} %copy.87.vec_ref, f32[256,256]{1,0:T(8,128)} %w_in_ref.1, f32[256,256]{1,0:T(8,128)} %w_out_ref.1), custom_call_target="tpu_custom_call" | custom-call | tf_op jit(solution)/shard_map/mlp/pallas_call | solution.py:208
  (74 shorter events, 3.1 us)
Async XLA Ops:
  0.0 274.3 %copy-start = (f32[256,256]{1,0:T(8,128)S(1)}, f32[256,256]{1,0:T(8,128)}, u32[]{:S(2)}) copy-start(f32[256,256]{1,0:T(8,128)} %param.12) | copy-start | bytes 786436
  11.7 190.5 %all-to-all-start = ((f32[32,16,32,128]{3,1,0,2:T(8,128)}), f32[32,16,32,128]{3,1,0,2:T(8,128)}, u32[]{:S(2)}, u32[]{:S(2)}) async-start(f32[32,16,32,128]{3,1,0,2:T(8,128)} %copy.83), calls=%async_computation | async-start | bytes 16777216 | tf_op jit(solution)/shard_map/all_to_all | solution.py:107
  18.4 0.6 copy-start.6
  36.8 9.9 %copy-start.9 = (f32[256,32]{0,1:T(8,128)S(1)}, f32[256,32]{0,1:T(8,128)}, u32[]{:S(2)}) copy-start(f32[256,32]{0,1:T(8,128)} %param.14) | copy-start | bytes 98308
  36.8 9.9 %copy-start.10 = (f32[256,32]{0,1:T(8,128)S(1)}, f32[256,32]{0,1:T(8,128)}, u32[]{:S(2)}) copy-start(f32[256,32]{0,1:T(8,128)} %param.13) | copy-start | bytes 98308
  44.3 81.4 %collective-permute-start = (f32[1088,512]{1,0:T(8,128)}, f32[1088,512]{1,0:T(8,128)}, u32[]{:S(2)}, u32[]{:S(2)}) collective-permute-start(f32[1088,512]{1,0:T(8,128)} %reshape.356), channel_id=1, source_target_pairs={{0,2},{2,0},{1,3},{3,1},{4,6},{6,4},{5,7},{7,5},{8,10},{10,8},{9,1... | collective-permute-start | bytes 6684680 | tf_op jit(solution)/shard_map/ppermute | solution.py:132
  96.4 1.1 copy-start.8
  96.4 1.2 copy-start.14
  116.0 9.8 %copy-start.1 = (f32[512,1024]{0,1:T(8,128)S(1)}, f32[512,1024]{0,1:T(8,128)}, u32[]{:S(2)}) copy-start(f32[512,1024]{0,1:T(8,128)} %div.43) | copy-start | bytes 6291460
  116.0 9.8 %copy-start.2 = (f32[512,1024]{0,1:T(8,128)S(1)}, f32[512,1024]{0,1:T(8,128)}, u32[]{:S(2)}) copy-start(f32[512,1024]{0,1:T(8,128)} %div.45) | copy-start | bytes 6291460
  162.4 4.9 %copy-start.3 = (f32[1024,512]{0,1:T(8,128)S(1)}, f32[1024,512]{0,1:T(8,128)}, u32[]{:S(2)}) copy-start(f32[1024,512]{0,1:T(8,128)} %add.216) | copy-start | bytes 6291460
  162.4 4.9 %copy-start.5 = (f32[1024,512]{0,1:T(8,128)S(1)}, f32[1024,512]{0,1:T(8,128)}, u32[]{:S(2)}) copy-start(f32[1024,512]{0,1:T(8,128)} %sub.36) | copy-start | bytes 6291460
  167.3 3.8 %copy-start.4 = (f32[1024,512]{0,1:T(8,128)S(1)}, f32[1024,512]{0,1:T(8,128)}, u32[]{:S(2)}) copy-start(f32[1024,512]{0,1:T(8,128)} %neg.22) | copy-start | bytes 6291460
  288.1 38.9 %copy-start.11 = (f32[256]{0:T(256)S(1)}, f32[256]{0:T(256)}, u32[]{:S(2)}) copy-start(f32[256]{0:T(256)} %param.16) | copy-start | bytes 3076
  288.1 38.9 %copy-start.7 = (f32[256]{0:T(256)S(1)}, f32[256]{0:T(256)}, u32[]{:S(2)}) copy-start(f32[256]{0:T(256)} %param.21) | copy-start | bytes 3076
  288.1 38.9 %copy-start.12 = (f32[256]{0:T(256)S(1)}, f32[256]{0:T(256)}, u32[]{:S(2)}) copy-start(f32[256]{0:T(256)} %param.17) | copy-start | bytes 3076
  288.1 38.9 %copy-start.13 = (f32[256]{0:T(256)S(1)}, f32[256]{0:T(256)}, u32[]{:S(2)}) copy-start(f32[256]{0:T(256)} %param.19) | copy-start | bytes 3076
